TPU v7x, 256 devices: a whole 4x4x8 slice. The times are simulated.
256 devices in a mesh: img: 16 (over y, x), row: 16 (over z, core).
Axes of the slice: x: 4, y: 4, z: 8, core: 2. Of those that a mesh axis runs over, the one named last changes fastest.
Arguments:
- latent: bfloat16 [1024, 128, 512], P(('img', 'row')), parts along dimension 0, may hold values from -8 to 8
- attn_gain: float32 [512], replicated, may hold values from 0.5 to 1.5
- attn_shift: float32 [512], replicated, may hold values from -3 to 3
- w_query: bfloat16 [512, 512], replicated, may hold values from -2 to 2
- w_key: bfloat16 [512, 512], replicated, may hold values from -2 to 2
- w_value: bfloat16 [512, 512], replicated, may hold values from -0.25 to 0.25
- w_out: bfloat16 [512, 512], replicated, may hold values from -0.25 to 0.25
- conv_gain: float32 [512], replicated, may hold values from 0.5 to 1.5
- conv_shift: float32 [512], replicated, may hold values from -3 to 3
- w_conv: bfloat16 [3, 3, 512, 512], replicated, may hold values from -0.09375 to 0.09375
- conv_bias: float32 [512], replicated, may hold values from -3 to 3
Outputs:
- encoded: bfloat16 [1024, 128, 512], P(('img', 'row')), parts along dimension 0
There are 16 independent parts, one for each index of `img`. A program takes and returns all parts, laid end to end along the dimension named above; an argument that names none is the same for every part. Nothing has to cross between parts.
All inputs are finite; a program needn't handle non-finite values.
Results may differ from a plain program's by a relative error of at most 0.011.
Values may be sent and summed in bfloat16 or wider, within the bound.
A program may use at most 128 MiB of HBM per device.

v0:
```python
import jax
import jax.numpy as jnp
from jax import lax
from jax.sharding import PartitionSpec as P

C = 512
GROUPS = 32
W = 128


epsilon = 1e-06


def copy_for_each(shard, axis):
    copies = jnp.broadcast_to(shard, (lax.axis_size(axis), *shard.shape))
    return lax.all_to_all(copies, axis, split_axis=0, concat_axis=0, tiled=True)


def taken_together(shard, axis):
    return copy_for_each(shard, axis).sum(axis=0)


def together(arrays, axis):
    line, at, done = (jnp.concatenate([a.reshape(-1) for a in arrays]), 0, [])
    total = taken_together(line, axis)
    for a in arrays:
        done.append(total[at : at + a.size].reshape(a.shape))
        at += a.size
    return tuple(done)


def with_halo(cells, sides, width):
    for axis, dim in sides:
        count = lax.axis_size(axis)
        ends = count - 1
        head = lax.slice_in_dim(cells, 0, width, axis=dim)
        tail = lax.slice_in_dim(cells, cells.shape[dim] - width, cells.shape[dim], axis=dim)
        cells = jnp.concatenate(
            [
                lax.ppermute(tail, axis, [(i, (i + 1) % count) for i in range(ends)]),
                cells,
                lax.ppermute(head, axis, [((i + 1) % count, i) for i in range(ends)]),
            ],
            axis=dim,
        )
    return cells


def group_stats(grouped, count):
    first, second = together(
        (jnp.sum(grouped, axis=(0, 2)), jnp.sum(grouped * grouped, axis=(0, 2))), "row"
    )
    centre = first / count
    spread = second / count - centre * centre
    return (centre, spread)


def group_norm(field, gain, shift):
    grouped = field.reshape(field.shape[0], GROUPS, C // GROUPS)
    count = field.shape[0] * lax.axis_size("row") * (C // GROUPS)
    centre, spread = group_stats(grouped, count)
    normed = (grouped - centre[None, :, None]) * lax.rsqrt(spread + epsilon)[None, :, None]
    return normed.reshape(field.shape) * gain + shift


def attend(carry, key_piece, value_piece, queries):
    maxima, denominator, accumulated = carry
    scaling = 1.0 / jnp.sqrt(jnp.float32(C))
    scores = (
        jnp.einsum("qc,kc->qk", queries, key_piece, preferred_element_type=jnp.float32) * scaling
    )
    newest = jnp.maximum(maxima, jnp.max(scores, axis=1))
    expo = jnp.exp(scores - newest[:, None])
    denominator = jnp.sum(expo, axis=1)
    accumulated = jnp.dot(
        expo.astype(jnp.bfloat16), value_piece, preferred_element_type=jnp.float32
    )
    return (newest, denominator, accumulated)


def local(
    latent,
    attn_gain,
    attn_shift,
    w_query,
    w_key,
    w_value,
    w_out,
    conv_gain,
    conv_shift,
    w_conv,
    conv_bias,
):
    local_rows = latent.shape[0]
    positions = latent.reshape(local_rows * W, C)
    normed = group_norm(positions.astype(jnp.float32), attn_gain, attn_shift).astype(jnp.bfloat16)
    queries = jnp.dot(normed, w_query, preferred_element_type=jnp.float32).astype(jnp.bfloat16)
    count_rows = positions.shape[0]
    start_carry = (
        jnp.full((count_rows,), -1e30, jnp.float32),
        jnp.zeros((count_rows,), jnp.float32),
        jnp.zeros((count_rows, C), jnp.float32),
    )
    piece = lax.all_gather(normed, "row", axis=0, tiled=True)
    key_piece = jnp.dot(piece, w_key, preferred_element_type=jnp.float32).astype(jnp.bfloat16)
    value_piece = jnp.dot(piece, w_value, preferred_element_type=jnp.float32).astype(jnp.bfloat16)
    maxima, denominator, accumulated = attend(start_carry, key_piece, value_piece, queries)
    attended = (accumulated / denominator[:, None]).astype(jnp.bfloat16)
    hidden = (
        positions.astype(jnp.float32) + jnp.dot(attended, w_out, preferred_element_type=jnp.float32)
    ).astype(jnp.bfloat16)
    activated = jax.nn.silu(group_norm(hidden.astype(jnp.float32), conv_gain, conv_shift)).astype(
        jnp.bfloat16
    )
    activated = activated.reshape(local_rows, W, C)
    bordered = with_halo(activated, (("row", 0),), 1)
    padded = jnp.pad(bordered, ((0, 0), (1, 1), (0, 0)))
    convolved = jnp.zeros((local_rows * W, C), jnp.float32)
    for row_tap in range(3):
        for col_tap in range(3):
            window = padded[row_tap : row_tap + local_rows, col_tap : col_tap + W].reshape(
                local_rows * W, C
            )
            convolved = convolved + jnp.dot(
                window, w_conv[row_tap, col_tap], preferred_element_type=jnp.float32
            )
    encoded = hidden.astype(jnp.float32) + (convolved + conv_bias)
    return encoded.astype(jnp.bfloat16).reshape(local_rows, W, C)


def solution(mesh):
    in_specs = (P(("img", "row"), None, None), P(), P(), P(), P(), P(), P(), P(), P(), P(), P())
    out_specs = P(("img", "row"), None, None)
    return jax.shard_map(local, mesh=mesh, in_specs=in_specs, out_specs=out_specs, check_vma=False)
```

profile of v0, /device:TPU:1, one launch (start us, length us, event | category | flops | bytes accessed | tf_op | source)
XLA Modules:
  0.0 157.1 jit_solution(7887998248014053439)
XLA Ops:
  6.5 1.3 convert_reduce_fusion.1
  7.8 0.1 reduce_sum.74
  7.9 0.1 reduce_sum.80
  8.0 0.1 reduce_sum.75
  8.1 0.1 reduce_sum.96
  8.2 0.1 pad_maximum_fusion.2
  8.3 16.8 %all_to_all.12 = f32[16,1,64]{2,1,0:T(1,128)S(1)} all-to-all(f32[16,1,64]{2,1,0:T(1,128)S(1)} %broadcast_in_dim.6), channel_id=1, replica_groups=mesh['img'=16,'row'=16] {'row'}, dimensions={0} | all-to-all | bytes 8192 | tf_op jit(solution)/shard_map/all_to_all | solution.py:16
  25.1 0.1 slice_multiply_fusion.1
  25.2 0.1 sub.40
  25.3 0.1 sub.41
  25.4 0.1 mul.68
  25.4 0.1 mul.69
  25.5 2.1 %fusion.31 = bf16[512,512]{1,0:T(8,128)(2,1)} fusion(bf16[4,128,512]{2,1,0:T(8,128)(2,1)} %param.11, f32[512]{0:T(512)} %param.13, f32[512]{0:T(512)} %param.12, f32[512]{0:T(512)S(1)} %mul.69, f32[512]{0:T(512)S(1)} %sub.41), kind=kLoop, calls=%fused_computation.46 | loop fusion | flops 1572864 | bytes 1056768 | tf_op jit(solution)/shard_map/convert_element_type | solution.py:96
  27.6 0.0 all-gather.2.cloned.1.call-update
  27.6 1.6 %convolution_convert_fusion.2 = bf16[512,512]{1,0:T(8,128)(2,1)S(1)} fusion(bf16[512,512]{1,0:T(8,128)(2,1)} %fusion.31, bf16[512,512]{1,0:T(8,128)(2,1)} %param.14), kind=kOutput, calls=%fused_computation.28 | convolution fusion | flops 268697600 | bytes 1572864 | tf_op jit(solution)/shard_map/dot_general | solution.py:97
  29.2 51.1 %all-gather.2.cloned.1.call-done = bf16[8192,512]{1,0:T(8,128)(2,1)} async-done(((bf16[512,512]{1,0:T(8,128)(2,1)}), bf16[8192,512]{1,0:T(8,128)(2,1)}) %all-gather.2.cloned.1.call-update) | async-done | bytes 8388624 | tf_op jit(solution)/shard_map/all_gather | solution.py:104
  80.4 14.5 %multiply_reduce_fusion = (f32[512]{0:T(512)S(1)}, f32[512,8192]{1,0:T(8,128)}) fusion(bf16[512,512]{1,0:T(8,128)(2,1)S(1)} %convolution_convert_fusion.2, bf16[8192,512]{1,0:T(8,128)(2,1)} %all-gather.2.cloned.1.call-done, bf16[512,512]{1,0:T(8,128)(2,1)S(1)} %copy-done), kind=kOutput, calls=%fused_computation.1 | convolution fusion | flops 8602517504 | bytes 26216448 | tf_op jit(solution)/shard_map/qc,kc->qk/dot_general | solution.py:70
  94.9 8.7 %fusion = f32[512]{0:T(512)S(1)} fusion(f32[512,8192]{1,0:T(8,128)} %get-tuple-element.24, f32[512]{0:T(512)S(1)} %broadcast_maximum_fusion), kind=kLoop, calls=%fused_computation.2 | loop fusion | flops 12582400 | bytes 16781312 | tf_op jit(solution)/shard_map/reduce_sum | solution.py:74
  103.6 17.2 %fusion.15 = bf16[512,512]{1,0:T(8,128)(2,1)S(1)} fusion(bf16[8192,512]{1,0:T(8,128)(2,1)} %all-gather.2.cloned.1.call-done, bf16[512,512]{1,0:T(8,128)(2,1)S(1)} %copy-done.5, f32[512,8192]{1,0:T(8,128)} %get-tuple-element.24, f32[512]{0:T(512)S(1)} %broadcast_maximum_fusion, f32[512]{0:T(512)S(1)} %fusion), kind=kOutput, calls=%fused_computation.31 | convolution fusion | flops 8607236096 | bytes 26218496 | tf_op jit(solution)/shard_map/dot_general | solution.py:75
  120.8 0.5 convert_reduce_fusion
  121.3 0.1 reduce_sum.100
  121.4 0.3 reduce_sum.101
  121.7 0.1 reduce_sum.103
  121.8 0.1 reduce_sum.104
  121.9 0.1 pad_maximum_fusion.3
  122.0 11.4 %all_to_all.13 = f32[16,1,64]{2,1,0:T(1,128)S(1)} all-to-all(f32[16,1,64]{2,1,0:T(1,128)S(1)} %broadcast_in_dim.8), channel_id=1, replica_groups=mesh['img'=16,'row'=16] {'row'}, dimensions={0} | all-to-all | bytes 8192 | tf_op jit(solution)/shard_map/all_to_all | solution.py:16
  133.4 0.1 slice_multiply_fusion
  133.5 0.1 sub.47
  133.6 0.1 sub.48
  133.7 0.1 mul.78
  133.7 0.1 mul.79
  133.8 0.4 fusion.27
  134.2 2.7 %collective-permute-start = (bf16[1,128,512]{2,1,0:T(8,128)(2,1)S(1)}, bf16[1,128,512]{2,1,0:T(8,128)(2,1)S(1)}, u32[]{:S(2)}, u32[]{:S(2)}) collective-permute-start(bf16[1,128,512]{2,1,0:T(8,128)(2,1)S(1)} %get-tuple-element.17), channel_id=1, source_target_pairs={{0,1},{1,2},{2,3},{3,4},{4,5},{5,6},{6,7},{7,8},{8,9},{9,10},{10,1... | collective-permute-start | bytes 393224 | tf_op jit(solution)/shard_map/ppermute | solution.py:40
  137.0 1.9 %collective-permute-start.1 = (bf16[1,128,512]{2,1,0:T(8,128)(2,1)S(1)}, bf16[1,128,512]{2,1,0:T(8,128)(2,1)S(1)}, u32[]{:S(2)}, u32[]{:S(2)}) collective-permute-start(bf16[1,128,512]{2,1,0:T(8,128)(2,1)S(1)} %get-tuple-element.18), channel_id=1, source_target_pairs={{1,0},{2,1},{3,2},{4,3},{5,4},{6,5},{7,6},{8,7},{9,8},{10,9},{11,1... | collective-permute-start | bytes 393224 | tf_op jit(solution)/shard_map/ppermute | solution.py:42
  138.9 4.3 %collective-permute-done.1 = bf16[1,128,512]{2,1,0:T(8,128)(2,1)S(1)} collective-permute-done((bf16[1,128,512]{2,1,0:T(8,128)(2,1)S(1)}, bf16[1,128,512]{2,1,0:T(8,128)(2,1)S(1)}, u32[]{:S(2)}, u32[]{:S(2)}) %collective-permute-start.1) | collective-permute-done | bytes 131104 | tf_op jit(solution)/shard_map/ppermute | solution.py:42
  143.3 0.2 fusion.36
  143.5 0.4 fusion.58
  143.9 1.7 %fusion.46 = f32[512,512]{1,0:T(8,128)S(1)} fusion(bf16[512,512]{1,0:T(8,128)(2,1)S(1)} %bitcast.82, bf16[3,3,512,512]{3,2,1,0:T(8,128)(2,1)} %param.20), kind=kOutput, calls=%fused_computation.65 | convolution fusion | flops 268435456 | bytes 2097152 | tf_op jit(solution)/shard_map/dot_general | solution.py:124
  145.6 0.1 pad_maximum_fusion
  145.7 0.1 slice-done.1
  145.8 0.4 convolution_add_fusion.6
  146.3 0.4 convolution_add_fusion.5
  146.7 0.4 convolution_add_fusion.4
  147.2 0.4 convolution_add_fusion.3
  147.6 0.4 fusion.37
  148.1 0.4 convolution_add_fusion.2
  148.5 0.4 convolution_add_fusion.1
  149.0 1.3 fusion.10
  (26 shorter events, 0.1 us)
Async XLA Ops:
  6.5 73.8 %copy-start = (bf16[512,512]{1,0:T(8,128)(2,1)S(1)}, bf16[512,512]{1,0:T(8,128)(2,1)}, u32[]{:S(2)}) copy-start(bf16[512,512]{1,0:T(8,128)(2,1)} %param.15) | copy-start | bytes 1572868
  6.5 73.8 %all-gather.2.cloned.1.call-start = ((), (), s32[]{:S(2)}) async-start(), calls=%async_computation.2 | async-start | bytes 8912896 | tf_op jit(solution)/shard_map/all_gather | solution.py:104
  94.9 8.7 %copy-start.5 = (bf16[512,512]{1,0:T(8,128)(2,1)S(1)}, bf16[512,512]{1,0:T(8,128)(2,1)}, u32[]{:S(2)}) copy-start(bf16[512,512]{1,0:T(8,128)(2,1)} %param.16) | copy-start | bytes 1572868
  103.6 17.2 %copy-start.1 = (bf16[4,128,512]{2,1,0:T(8,128)(2,1)S(1)}, bf16[4,128,512]{2,1,0:T(8,128)(2,1)}, u32[]{:S(2)}) copy-start(bf16[4,128,512]{2,1,0:T(8,128)(2,1)} %param.11) | copy-start | bytes 1572868
  103.6 17.2 %copy-start.6 = (bf16[512,512]{1,0:T(8,128)(2,1)S(1)}, bf16[512,512]{1,0:T(8,128)(2,1)}, u32[]{:S(2)}) copy-start(bf16[512,512]{1,0:T(8,128)(2,1)} %param.17) | copy-start | bytes 1572868
  103.6 30.2 %copy-start.2 = (f32[512]{0:T(512)S(1)}, f32[512]{0:T(512)}, u32[]{:S(2)}) copy-start(f32[512]{0:T(512)} %param.19) | copy-start | bytes 6148
  103.6 30.2 %copy-start.3 = (f32[512]{0:T(512)S(1)}, f32[512]{0:T(512)}, u32[]{:S(2)}) copy-start(f32[512]{0:T(512)} %param.18) | copy-start | bytes 6148
  120.8 24.9 %slice-start = ((s8[4718592]{0:T(1024)(128)(4,1)}), s8[524288]{0:T(1024)(128)(4,1)S(1)}, s32[]{:S(2)}) async-start(s8[4718592]{0:T(1024)(128)(4,1)} %bitcast.74), calls=%async_computation.3 | async-start | bytes 1048576
  134.2 4.7 %collective-permute-start = (bf16[1,128,512]{2,1,0:T(8,128)(2,1)S(1)}, bf16[1,128,512]{2,1,0:T(8,128)(2,1)S(1)}, u32[]{:S(2)}, u32[]{:S(2)}) collective-permute-start(bf16[1,128,512]{2,1,0:T(8,128)(2,1)S(1)} %get-tuple-element.17), channel_id=1, source_target_pairs={{0,1},{1,2},{2,3},{3,4},{4,5},{5,6},{6,7},{7,8},{8,9},{9,10},{10,1... | collective-permute-start | bytes 393224 | tf_op jit(solution)/shard_map/ppermute | solution.py:40
  137.0 6.3 %collective-permute-start.1 = (bf16[1,128,512]{2,1,0:T(8,128)(2,1)S(1)}, bf16[1,128,512]{2,1,0:T(8,128)(2,1)S(1)}, u32[]{:S(2)}, u32[]{:S(2)}) collective-permute-start(bf16[1,128,512]{2,1,0:T(8,128)(2,1)S(1)} %get-tuple-element.18), channel_id=1, source_target_pairs={{1,0},{2,1},{3,2},{4,3},{5,4},{6,5},{7,6},{8,7},{9,8},{10,9},{11,1... | collective-permute-start | bytes 393224 | tf_op jit(solution)/shard_map/ppermute | solution.py:42
  143.5 2.3 %slice-start.1 = ((s8[4718592]{0:T(1024)(128)(4,1)}), s8[4194304]{0:T(1024)(128)(4,1)S(1)}, s32[]{:S(2)}) async-start(s8[4718592]{0:T(1024)(128)(4,1)} %bitcast.74), calls=%async_computation.4 | async-start | bytes 8388608
  146.3 2.7 %copy-start.4 = (f32[512]{0:T(512)S(1)}, f32[512]{0:T(512)}, u32[]{:S(2)}) copy-start(f32[512]{0:T(512)} %param.21) | copy-start | bytes 6148
Sparse Core Ops, SparseCore 0:
  27.7 52.6 all-gather.1
where the time goes:
time: 157 us
  waiting for transfers between devices  55.5 us (35%)
  matrix products  39.9 us (25%)
  blocking collectives  28.2 us (18%)
  other arithmetic  13.7 us (9%)
  between operations  13.6 us (9%)
  starting transfers between devices  4.64 us (3%)
    all_gather x1, waiting for transfers between devices, local(): piece = lax.all_gather(normed, 'row', axis=0, tiled=True)  51.1 us
    all_to_all x2, blocking collectives, copy_for_each(): return lax.all_to_all(copies, axis, split_axis=0, concat_axis=0, tiled=True)  28.2 us
    dot_general x1, matrix products, attend(): jnp.dot(expo.astype(jnp.bfloat16), value_piece, preferred_element_type=jn...  17.2 us
    dot_general x1, matrix products, attend(): jnp.einsum('qc,kc->qk', queries, key_piece, preferred_element_type=jnp.fl...  14.5 us
    reduce_sum x1, other arithmetic, attend(): denominator = jnp.sum(expo, axis=1)  8.68 us
    dot_general x9, matrix products, local(): jnp.dot(window, w_conv[row_tap, col_tap], preferred_element_type=jnp.floa...  6.07 us
    ppermute x1, waiting for transfers between devices, with_halo(): lax.ppermute(head, axis, [((i + 1) % count, i) for i in range(ends)])  4.35 us
  transfers between devices with their start and end apart: 3, of which 2 were waited for; matrix products, arithmetic and copies ran while one was open for 1% of the time, Pallas kernels for 0%

commit v1 on v0

v1 whole, which is shorter than its diff:
```python
import jax
import jax.numpy as jnp
from jax import lax
from jax.experimental import pallas as pl
from jax.experimental.pallas import tpu as pltpu
from jax.sharding import PartitionSpec as P

C = 512
W = 128
ROWS = 4
N = ROWS * W
CH = 128
GROUP = 16
DEV = 16
ZN = 8
SENDS = 14
EPS = 1e-06
F32 = jnp.float32
BF16 = jnp.bfloat16
LOG2E = 1.4426950408889634

NT = (((1,), (1,)), ((), ()))


def dot(a, b, dims=(((1,), (0,)), ((), ()))):
    return lax.dot_general(a, b, dims, preferred_element_type=F32)


def group_total(v):
    lane = lax.broadcasted_iota(jnp.int32, v.shape, v.ndim - 1)
    step = 1
    while step < GROUP:
        up = pltpu.roll(v, 128 - step, v.ndim - 1)
        down = pltpu.roll(v, step, v.ndim - 1)
        v = v + jnp.where((lane // step) % 2 == 0, up, down)
        step *= 2
    return v


def as_line(v):
    return jnp.concatenate([v[i : i + 1, :] for i in range(4)], axis=1)


def local_moments(read, buf):
    total = jnp.zeros((8, C), F32)
    for i in range(4):
        part = read(i).astype(F32).reshape(CH // 8, 8, C)
        total = total + jnp.sum(part, axis=0)
    mean = jnp.sum(total, axis=0, keepdims=True) * (1.0 / N)
    dev = jnp.zeros((8, C), F32)
    for i in range(4):
        off = read(i).astype(F32).reshape(CH // 8, 8, C) - mean[None]
        dev = dev + jnp.sum(off * off, axis=0)
    dev = jnp.sum(dev, axis=0, keepdims=True)
    for i in range(4):
        buf[i : i + 1, :] = mean[:, 128 * i : 128 * i + 128]
        buf[4 + i : 5 + i, :] = dev[:, 128 * i : 128 * i + 128]


def combined(stats, own):
    means = [own[0:4, :]]
    devs = [own[4:8, :]]
    for i in range(DEV - 1):
        means.append(stats[i, 0:4, :])
        devs.append(stats[i, 4:8, :])
    centre = group_total(sum(means[1:], means[0])) * (1.0 / (DEV * GROUP))
    spread = jnp.zeros((4, 128), F32)
    for m, d in zip(means, devs):
        off = m - centre
        spread = spread + (d + float(N) * (off * off))
    spread = group_total(spread) * (1.0 / (DEV * GROUP * N))
    return as_line(centre), as_line(lax.rsqrt(spread + EPS))


def kernel(
    x_hbm, ag_h, as_h, wq_h, wk_h, wv_h, wo_h, cg_h, cs_h, wc_h, cb_h,
    out_ref,
    kv, wq, wk, wv, wo, wc, vecs, q_s, acc, m_s, l_s, hid, halo, lhs, mine, stat_a, stat_b,
    load_sem, w_sem, wc_sem, v_sem,
    ring_send, ring_recv, sib_send, sib_recv, own_send, own_recv,
    sa_send, sa_recv, sb_send, sb_recv, h_send, h_recv,
):
    me = lax.axis_index("row")
    z = me // 2
    core = me % 2
    right = ((z + 1) % ZN) * 2 + core
    left = ((z + ZN - 1) % ZN) * 2 + core
    sib = z * 2 + (1 - core)

    loads = [
        pltpu.make_async_copy(x_hbm.at[pl.ds(CH * i, CH)], kv.at[me, i], load_sem.at[i])
        for i in range(4)
    ]
    for c in loads:
        c.start()

    barrier = pltpu.get_barrier_semaphore()
    for d in range(1, DEV):
        pl.semaphore_signal(barrier, inc=1, device_id={"row": (me + d) % DEV})

    small = [
        pltpu.make_async_copy(src, vecs.at[i], v_sem.at[i])
        for i, src in enumerate((ag_h, as_h, cg_h, cs_h, cb_h))
    ]
    for c in small:
        c.start()
    weights = [
        pltpu.make_async_copy(src, dst, w_sem.at[i])
        for i, (src, dst) in enumerate(((wq_h, wq), (wk_h, wk), (wv_h, wv), (wo_h, wo)))
    ]
    for c in weights:
        c.start()
    taps = [
        pltpu.make_async_copy(
            wc_h.at[dy, dx], wc.at[dx, pl.ds(C * dy, C)], wc_sem.at[3 * dy + dx]
        )
        for dy in range(3)
        for dx in range(3)
    ]
    for c in taps:
        c.start()

    def ring(way, blk, chunk, j):
        return pltpu.make_async_remote_copy(
            src_ref=kv.at[blk, chunk],
            dst_ref=kv.at[blk, chunk],
            send_sem=ring_send.at[way, j],
            recv_sem=ring_recv.at[way, j],
            device_id={"row": right if way == 0 else left},
        )

    def to_sib(blk, chunk, sends, recvs):
        return pltpu.make_async_remote_copy(
            src_ref=kv.at[blk, chunk],
            dst_ref=kv.at[blk, chunk],
            send_sem=sends,
            recv_sem=recvs,
            device_id={"row": sib},
        )

    def stat_copy(d, dst, sends, recvs):
        return pltpu.make_async_remote_copy(
            src_ref=mine,
            dst_ref=dst.at[d - 1],
            send_sem=sends.at[d - 1],
            recv_sem=recvs.at[d - 1],
            device_id={"row": (me + d) % DEV},
        )

    pl.semaphore_wait(barrier, DEV - 1)

    order = ((0, 2), (1, 3), (2, 0), (3, 1))
    loads[0].wait()
    ring(0, me, 0, 0).start()
    loads[2].wait()
    ring(1, me, 2, 0).start()
    loads[1].wait()
    loads[3].wait()

    local_moments(lambda i: kv[me, i], mine)
    for d in range(1, DEV):
        stat_copy(d, stat_a, sa_send, sa_recv).start()
    for j in range(1, 4):
        ring(0, me, order[j][0], j).start()
        ring(1, me, order[j][1], j).start()
    for i in range(4):
        to_sib(me, i, own_send.at[i], own_recv.at[i]).start()

    m_s[...] = jnp.full_like(m_s, -1e30)
    l_s[...] = jnp.zeros_like(l_s)
    acc[...] = jnp.zeros_like(acc)

    for c in weights:
        c.wait()
    wv[...] = dot(wv[...], wo[...]).astype(BF16)

    def came(i):
        chunk = i % 4
        far = i // 4 + 1
        blk_r = ((z + ZN - far) % ZN) * 2 + core
        blk_l = ((z + far) % ZN) * 2 + core
        return blk_r, chunk, blk_l, (chunk + 2) % 4

    def comm(i):
        blk_r, cr, blk_l, cl = came(i)
        ring(0, blk_r, cr, i).wait_recv()
        ring(1, blk_l, cl, i).wait_recv()

        @pl.when(i < SENDS - 4)
        def _():
            ring(0, blk_r, cr, i + 4).start()
            ring(1, blk_l, cl, i + 4).start()

        to_sib(blk_r, cr, sib_send.at[0, i], sib_recv.at[0, i]).start()
        to_sib(blk_l, cl, sib_send.at[1, i], sib_recv.at[1, i]).start()

    def attend(blk_a, ca, blk_b, cb):
        keys = jnp.concatenate([kv[blk_a, ca], kv[blk_b, cb]], axis=0)
        for t in range(2):
            rows = pl.ds(256 * t, 256)
            s = dot(q_s[rows, :], keys, NT)
            m_old = m_s[rows, :]
            m_new = jnp.maximum(m_old, jnp.max(s, axis=1, keepdims=True))
            alpha = jnp.exp2(m_old - m_new)
            p0 = jnp.exp2(s[:, :128] - m_new).astype(BF16)
            p1 = jnp.exp2(s[:, 128:] - m_new).astype(BF16)
            l_s[rows, :] = l_s[rows, :] * alpha + (p0.astype(F32) + p1.astype(F32))
            m_s[rows, :] = m_new
            pv = dot(jnp.concatenate([p0, p1], axis=1), keys)
            acc[rows, :] = acc[rows, :] * jnp.concatenate([alpha] * 4, axis=1) + pv

    comm(0)

    for c in small:
        c.wait()
    for d in range(1, DEV):
        stat_copy(d, stat_a, sa_send, sa_recv).wait()
    mean, rs = combined(stat_a, mine)
    scale = rs * vecs[0]
    shift = vecs[1]
    for i in range(4):
        normed = ((kv[me, i].astype(F32) - mean) * scale + shift).astype(BF16)
        query = dot(normed, wq[...]).astype(BF16)
        folded = dot(query, wk[...], NT) * (scale * (LOG2E / C**0.5))
        q_s[CH * i : CH * i + CH, :] = folded.astype(BF16)

    for i in range(4):
        to_sib(me, i, own_send.at[i], own_recv.at[i]).wait_recv()

    def first(k, carry):
        blk = jnp.where(k < 2, me, sib)
        attend(blk, 2 * (k % 2), blk, 2 * (k % 2) + 1)
        return carry

    lax.fori_loop(0, 4, first, 0)

    def other(i):
        blk_r, cr, blk_l, cl = came(i)
        return blk_r + 1 - 2 * core, cr, blk_l + 1 - 2 * core, cl

    def sib_wait(i):
        blk_r, cr, blk_l, cl = other(i)
        to_sib(blk_r, cr, sib_send.at[0, i], sib_recv.at[0, i]).wait_recv()
        to_sib(blk_l, cl, sib_send.at[1, i], sib_recv.at[1, i]).wait_recv()

    def body(i, carry):
        @pl.when(i > 0)
        def _():
            comm(i)
            sib_wait(i - 1)
            attend(*other(i - 1))

        attend(*came(i))
        return carry

    lax.fori_loop(0, SENDS, body, 0)
    sib_wait(SENDS - 1)
    attend(*other(SENDS - 1))

    for t in range(4):
        rows = pl.ds(CH * t, CH)
        inv = 1.0 / jnp.sum(l_s[rows, :], axis=1, keepdims=True)
        att = ((acc[rows, :] * inv - mean) * scale + shift).astype(BF16)
        hid[t] = (kv[me, t].astype(F32) + dot(att, wv[...])).astype(BF16)

    def halo_copy(k, row, peer):
        return pltpu.make_async_remote_copy(
            src_ref=hid.at[row],
            dst_ref=halo.at[k],
            send_sem=h_send.at[k],
            recv_sem=h_recv.at[k],
            device_id={"row": peer},
        )

    down = halo_copy(0, ROWS - 1, (me + 1) % DEV)
    up = halo_copy(1, 0, (me + DEV - 1) % DEV)
    down.start()
    up.start()
    local_moments(lambda i: hid[i], mine)
    for d in range(1, DEV):
        stat_copy(d, stat_b, sb_send, sb_recv).start()
    for c in taps:
        c.wait()
    down.wait()
    up.wait()
    for d in range(1, DEV):
        stat_copy(d, stat_b, sb_send, sb_recv).wait()
    mean2, rs2 = combined(stat_b, mine)
    scale2 = rs2 * vecs[2] * 0.5
    shift2 = vecs[3] * 0.5

    for j in range(ROWS + 2):
        src = halo[0] if j == 0 else halo[1] if j == ROWS + 1 else hid[j - 1]
        half = (src.astype(F32) - mean2) * scale2 + shift2
        act = half + half * jnp.tanh(half)
        if j == 0:
            act = jnp.where(me == 0, 0.0, act)
        if j == ROWS + 1:
            act = jnp.where(me == DEV - 1, 0.0, act)
        act = act.astype(BF16)
        for dy in range(3):
            i = j - dy
            if 0 <= i < ROWS:
                lhs[CH * i : CH * i + CH, C * dy : C * dy + C] = act

    col = lax.broadcasted_iota(jnp.int32, (N, 256), 0) % W
    for n in range(2):
        cols = slice(256 * n, 256 * n + 256)
        t0 = dot(lhs[...], wc[0, :, cols])
        t1 = dot(lhs[...], wc[1, :, cols])
        t2 = dot(lhs[...], wc[2, :, cols])
        total = t1 + jnp.where(col == 0, 0.0, pltpu.roll(t0, 1, 0))
        total = total + jnp.where(col == W - 1, 0.0, pltpu.roll(t2, N - 1, 0))
        base = jnp.concatenate([hid[i, :, cols] for i in range(4)], axis=0).astype(F32)
        out_ref[:, cols] = (base + (total + vecs[4, :, cols])).astype(BF16)

    def drain(i, carry):
        blk_r, cr, blk_l, cl = came(i)
        ring(0, blk_r, cr, i).wait_send()
        ring(1, blk_l, cl, i).wait_send()
        to_sib(blk_r, cr, sib_send.at[0, i], sib_recv.at[0, i]).wait_send()
        to_sib(blk_l, cl, sib_send.at[1, i], sib_recv.at[1, i]).wait_send()
        return carry

    lax.fori_loop(0, SENDS, drain, 0)
    for i in range(4):
        to_sib(me, i, own_send.at[i], own_recv.at[i]).wait_send()


def local(
    latent, attn_gain, attn_shift, w_query, w_key, w_value, w_out,
    conv_gain, conv_shift, w_conv, conv_bias,
):
    line = lambda v: v.reshape(1, C)
    dma = pltpu.SemaphoreType.DMA
    out = pl.pallas_call(
        kernel,
        out_shape=jax.ShapeDtypeStruct((N, C), BF16),
        in_specs=[pl.BlockSpec(memory_space=pl.ANY)] * 11,
        out_specs=pl.BlockSpec(memory_space=pltpu.VMEM),
        scratch_shapes=[
            pltpu.VMEM((DEV, 4, CH, C), BF16),
            pltpu.VMEM((C, C), BF16),
            pltpu.VMEM((C, C), BF16),
            pltpu.VMEM((C, C), BF16),
            pltpu.VMEM((C, C), BF16),
            pltpu.VMEM((3, 3 * C, C), BF16),
            pltpu.VMEM((5, 1, C), F32),
            pltpu.VMEM((N, C), BF16),
            pltpu.VMEM((N, C), F32),
            pltpu.VMEM((N, 128), F32),
            pltpu.VMEM((N, 128), F32),
            pltpu.VMEM((ROWS, W, C), BF16),
            pltpu.VMEM((2, W, C), BF16),
            pltpu.VMEM((N, 3 * C), BF16),
            pltpu.VMEM((8, 128), F32),
            pltpu.VMEM((DEV - 1, 8, 128), F32),
            pltpu.VMEM((DEV - 1, 8, 128), F32),
            dma((4,)),
            dma((4,)),
            dma((9,)),
            dma((5,)),
            dma((2, SENDS)),
            dma((2, SENDS)),
            dma((2, SENDS)),
            dma((2, SENDS)),
            dma((4,)),
            dma((4,)),
            dma((DEV - 1,)),
            dma((DEV - 1,)),
            dma((DEV - 1,)),
            dma((DEV - 1,)),
            dma((2,)),
            dma((2,)),
        ],
        compiler_params=pltpu.CompilerParams(
            collective_id=0, has_side_effects=True, vmem_limit_bytes=60 * 1024 * 1024
        ),
    )(
        latent.reshape(N, C), line(attn_gain), line(attn_shift), w_query, w_key, w_value, w_out,
        line(conv_gain), line(conv_shift), w_conv, line(conv_bias),
    )
    return out.reshape(ROWS, W, C)


def solution(mesh):
    part = P(("img", "row"), None, None)
    return jax.shard_map(
        local, mesh=mesh, in_specs=(part,) + (P(),) * 10, out_specs=part, check_vma=False
    )
```

time: 157 us -> 68.4 us (0.44)
  Pallas kernels: 0 us -> 66.4 us
  waiting for transfers between devices: 55.5 us -> 0 us
  matrix products: 39.9 us -> 0 us
  blocking collectives: 28.2 us -> 0 us
  other arithmetic: 13.7 us -> 0 us
  between operations: 13.6 us -> 0.01 us
  starting transfers between devices: 4.64 us -> 0 us
    pallas_call x0 -> x1, Pallas kernels: none -> 66.4 us  [local(): pl.pallas_call(kernel, out_shape=jax.ShapeDtypeStruct((N, C), BF16), in_s...]
    all_gather x1 -> x0, waiting for transfers between devices: 51.1 us -> none  [local(): piece = lax.all_gather(normed, 'row', axis=0, tiled=True)]
    dot_general x13 -> x0, matrix products: 39.9 us -> none  [the longest x1 17.2 us: attend(): jnp.dot(expo.astype(jnp.bfloat16), value_piece, preferred_element_type=jn...]
    all_to_all x2 -> x0, blocking collectives: 28.2 us -> none  [copy_for_each(): return lax.all_to_all(copies, axis, split_axis=0, concat_axis=0, tiled=True)]
    reduce_sum x8 -> x0, other arithmetic: 10.6 us -> none  [the longest x1 8.68 us: attend(): denominator = jnp.sum(expo, axis=1)]
    ppermute x2 -> x0, starting transfers between devices: 4.64 us -> none  [the longest x1 2.72 us: with_halo(): lax.ppermute(tail, axis, [(i, (i + 1) % count) for i in range(ends)])]
    ppermute x2 -> x0, waiting for transfers between devices: 4.35 us -> none  [the longest x1 4.35 us: with_halo(): lax.ppermute(head, axis, [((i + 1) % count, i) for i in range(ends)])]
    convert_element_type x2 -> x0, other arithmetic: 2.43 us -> none  [the longest x1 2.06 us: local(): group_norm(positions.astype(jnp.float32), attn_gain, attn_shift)]
  transfers between devices with their start and end apart: 3 -> 0, of which waited for: 2 -> 0; matrix products, arithmetic and copies ran while one was open for 1% -> 0% of each run, Pallas kernels for 0% -> 0%
where the time goes in v1:
time: 68.4 us; the launch traced here: 68.3 us
  Pallas kernels  66.4 us (97%)
  local copies, waits for them, and re-layouts  1.87 us (3%)
    pallas_call x1, Pallas kernels, local(): pl.pallas_call(kernel, out_shape=jax.ShapeDtypeStruct((N, C), BF16), in_s...  66.4 us
    unnamed x1, local copies, waits for them, and re-layouts  1.87 us

profile of v1, /device:TPU:1, one launch (start us, length us, event | category | flops | bytes accessed | tf_op | source)
XLA Modules:
  0.0 68.3 jit_solution(3685949438501524801)
XLA Ops:
  0.0 66.4 %shard_map.109 = bf16[512,512]{1,0:T(8,128)(2,1)} custom-call(bf16[512,512]{1,0:T(8,128)(2,1)} %bitcast.8, f32[1,512]{1,0:T(1,128)} %bitcast.9, f32[1,512]{1,0:T(1,128)} %bitcast.10, bf16[512,512]{1,0:T(8,128)(2,1)} %wq_h.1, bf16[512,512]{1,0:T(8,128)(2,1)} %wk_h.1, bf16[512,512]{1,0:T(8,128)(2,1)} %wv_h.1, bf16[512,512]{1,0:T(8,128)(2,1)} %wo_h.1, ...), custom_call_target="tpu_custom_call" | custom-call | tf_op jit(solution)/shard_map/pallas_call | solution.py:336
  66.4 1.9 %copy.13 = bf16[4,128,512]{2,1,0:T(8,128)(2,1)} copy(bf16[4,128,512]{2,1,0:T(8,128)(2,1)} %bitcast.7) | data formatting | bytes 1048576

commit v2 on v1

v2 whole, which is shorter than its diff:
```python
import jax
import jax.numpy as jnp
from jax import lax
from jax.experimental import pallas as pl
from jax.experimental.pallas import tpu as pltpu
from jax.sharding import PartitionSpec as P

C = 512
W = 128
ROWS = 4
N = ROWS * W
CH = 128
GROUP = 16
DEV = 16
ZN = 8
SENDS = 14
TILE = 256
EPS = 1e-06
F32 = jnp.float32
BF16 = jnp.bfloat16
LOG2E = 1.4426950408889634

NT = (((1,), (1,)), ((), ()))


def dot(a, b, dims=(((1,), (0,)), ((), ()))):
    return lax.dot_general(a, b, dims, preferred_element_type=F32)


def as_line(v):
    return jnp.concatenate([v[i : i + 1, :] for i in range(4)], axis=1)


def put_moments(first, total, square, buf):
    total = jnp.sum(total, axis=0, keepdims=True)
    square = jnp.sum(square, axis=0, keepdims=True)
    off = total * (1.0 / N)
    dev = jnp.maximum(square - total * off, 0.0)
    mean = first + off
    for i in range(4):
        buf[i : i + 1, :] = mean[:, 128 * i : 128 * i + 128]
        buf[4 + i : 5 + i, :] = dev[:, 128 * i : 128 * i + 128]


def sums_about(first, block):
    off = (block - first).reshape(block.shape[0] // 8, 8, C)
    return jnp.sum(off, axis=0), jnp.sum(off * off, axis=0)


def combined(stats, own):
    means = [own[0:4, :]] + [stats[i, 0:4, :] for i in range(DEV - 1)]
    devs = [own[4:8, :]] + [stats[i, 4:8, :] for i in range(DEV - 1)]
    centre = sum(means[1:], means[0]) * (1.0 / DEV)
    spread = jnp.zeros((4, 128), F32)
    for m, d in zip(means, devs):
        off = m - centre
        spread = spread + (d + float(N) * (off * off))
    lane = lax.broadcasted_iota(jnp.int32, (4, 128), 1)
    count = float(N * DEV)
    step = 1
    while step < GROUP:
        low = (lane // step) % 2 == 0
        both = []
        for v in (centre, spread):
            both.append(jnp.where(low, pltpu.roll(v, 128 - step, 1), pltpu.roll(v, step, 1)))
        gap = both[0] - centre
        spread = spread + both[1] + (0.5 * count) * (gap * gap)
        centre = 0.5 * (centre + both[0])
        step *= 2
        count *= 2.0
    return as_line(centre), as_line(lax.rsqrt(spread * (1.0 / count) + EPS))


def kernel(
    x_hbm, ag_h, as_h, wq_h, wk_h, wv_h, wo_h, cg_h, cs_h, wc_h,
    hid, edges, coef, wc,
    kv, wq, wk, wv, wo, vecs, q_s, acc, m_s, l_s, halo, mine, stat_a, stat_b,
    load_sem, w_sem, wc_sem, v_sem,
    ring_send, ring_recv, sib_send, sib_recv, own_send, own_recv,
    sa_send, sa_recv, sb_send, sb_recv, h_send, h_recv, known,
):
    me = lax.axis_index("row")
    z = me // 2
    core = me % 2
    right = ((z + 1) % ZN) * 2 + core
    left = ((z + ZN - 1) % ZN) * 2 + core
    sib = z * 2 + (1 - core)

    loads = [
        pltpu.make_async_copy(x_hbm.at[pl.ds(CH * i, CH)], kv.at[me, i], load_sem.at[i])
        for i in range(4)
    ]
    for c in loads:
        c.start()

    barrier = pltpu.get_barrier_semaphore()
    for peer in (left, right, sib):
        pl.semaphore_signal(barrier, inc=1, device_id={"row": peer})

    small = [
        pltpu.make_async_copy(src, vecs.at[i], v_sem.at[i])
        for i, src in enumerate((ag_h, as_h, cg_h, cs_h))
    ]
    for c in small:
        c.start()
    weights = [
        pltpu.make_async_copy(src, dst, w_sem.at[i])
        for i, (src, dst) in enumerate(((wq_h, wq), (wk_h, wk), (wv_h, wv), (wo_h, wo)))
    ]
    for c in weights:
        c.start()
    taps = [
        pltpu.make_async_copy(
            wc_h.at[dy, dx], wc.at[dx, pl.ds(C * dy, C)], wc_sem.at[3 * dy + dx]
        )
        for dy in range(3)
        for dx in range(3)
    ]
    for c in taps:
        c.start()

    def ring(way, blk, chunk, j):
        return pltpu.make_async_remote_copy(
            src_ref=kv.at[blk, chunk],
            dst_ref=kv.at[blk, chunk],
            send_sem=ring_send.at[way, j],
            recv_sem=ring_recv.at[way, j],
            device_id={"row": right if way == 0 else left},
        )

    def to_sib(blk, chunk, sends, recvs):
        return pltpu.make_async_remote_copy(
            src_ref=kv.at[blk, chunk],
            dst_ref=kv.at[blk, chunk],
            send_sem=sends,
            recv_sem=recvs,
            device_id={"row": sib},
        )

    def stat_copy(d, dst, sends, recvs):
        return pltpu.make_async_remote_copy(
            src_ref=mine,
            dst_ref=dst.at[d - 1],
            send_sem=sends.at[d - 1],
            recv_sem=recvs.at[d - 1],
            device_id={"row": (me + d) % DEV},
        )

    pl.semaphore_wait(barrier, 3)

    order = ((0, 2), (1, 3), (2, 0), (3, 1))
    loads[0].wait()
    ring(0, me, 0, 0).start()
    loads[2].wait()
    ring(1, me, 2, 0).start()
    loads[1].wait()
    loads[3].wait()
    ring(0, me, 1, 1).start()
    ring(1, me, 3, 1).start()

    far_right = ((z + 2) % ZN) * 2 + core
    far_left = ((z + ZN - 2) % ZN) * 2 + core
    for k, peers in enumerate(((left, right, sib), (far_left, far_right), (sib,))):
        for peer in peers:
            pl.semaphore_signal(known.at[k], inc=1, device_id={"row": peer})
        if k == 0:
            base = kv[me, 0, 0:1, :].astype(F32)
            sums = [sums_about(base, kv[me, i].astype(F32)) for i in range(4)]
            put_moments(base, sum(a for a, _ in sums), sum(b for _, b in sums), mine)
        pl.semaphore_wait(known.at[k], len(peers))

    for d in range(1, DEV):
        stat_copy(d, stat_a, sa_send, sa_recv).start()
    for j in range(2, 4):
        ring(0, me, order[j][0], j).start()
        ring(1, me, order[j][1], j).start()
    for i in range(4):
        to_sib(me, i, own_send.at[i], own_recv.at[i]).start()

    m_s[...] = jnp.full_like(m_s, -1e30)
    l_s[...] = jnp.zeros_like(l_s)
    acc[...] = jnp.zeros_like(acc)

    for c in weights:
        c.wait()
    wv[...] = dot(wv[...], wo[...]).astype(BF16)

    def came(i):
        chunk = i % 4
        far = i // 4 + 1
        blk_r = ((z + ZN - far) % ZN) * 2 + core
        blk_l = ((z + far) % ZN) * 2 + core
        return blk_r, chunk, blk_l, (chunk + 2) % 4

    def comm(i):
        blk_r, cr, blk_l, cl = came(i)
        ring(0, blk_r, cr, i).wait_recv()
        ring(1, blk_l, cl, i).wait_recv()

        @pl.when(i < SENDS - 4)
        def _():
            ring(0, blk_r, cr, i + 4).start()
            ring(1, blk_l, cl, i + 4).start()

        to_sib(blk_r, cr, sib_send.at[0, i], sib_recv.at[0, i]).start()
        to_sib(blk_l, cl, sib_send.at[1, i], sib_recv.at[1, i]).start()

    def attend(*chunks):
        keys = jnp.concatenate([kv[blk, chunk] for blk, chunk in chunks], axis=0)
        spans = range(0, CH * len(chunks), 128)

        def weigh(rows, s):
            m_old = m_s[rows, :]
            m_new = jnp.maximum(m_old, jnp.max(s, axis=1, keepdims=True))
            alpha = jnp.exp2(m_old - m_new)
            p = [jnp.exp2(s[:, k : k + 128] - m_new).astype(BF16) for k in spans]
            l_s[rows, :] = l_s[rows, :] * alpha + sum(v.astype(F32) for v in p)
            m_s[rows, :] = m_new
            return jnp.concatenate([alpha] * 4, axis=1), jnp.concatenate(p, axis=1)

        tiles = [pl.ds(TILE * t, TILE) for t in range(N // TILE)]
        s = dot(q_s[tiles[0], :], keys, NT)
        for t, rows in enumerate(tiles):
            ahead = dot(q_s[tiles[t + 1], :], keys, NT) if t + 1 < len(tiles) else None
            alpha, p = weigh(rows, s)
            acc[rows, :] = acc[rows, :] * alpha + dot(p, keys)
            s = ahead

    comm(0)

    for c in small:
        c.wait()
    for d in range(1, DEV):
        stat_copy(d, stat_a, sa_send, sa_recv).wait()
    mean, rs = combined(stat_a, mine)
    scale = rs * vecs[0]
    shift = vecs[1]
    for i in range(4):
        normed = ((kv[me, i].astype(F32) - mean) * scale + shift).astype(BF16)
        query = dot(normed, wq[...]).astype(BF16)
        folded = dot(query, wk[...], NT) * (scale * (LOG2E / C**0.5))
        q_s[CH * i : CH * i + CH, :] = folded.astype(BF16)

    for i in range(4):
        to_sib(me, i, own_send.at[i], own_recv.at[i]).wait_recv()

    def first(k, carry):
        blk = jnp.where(k < 1, me, sib)
        attend((blk, 0), (blk, 1), (blk, 2), (blk, 3))
        return carry

    lax.fori_loop(0, 2, first, 0)

    def other(i):
        blk_r, cr, blk_l, cl = came(i)
        return blk_r + 1 - 2 * core, cr, blk_l + 1 - 2 * core, cl

    def sib_wait(i):
        blk_r, cr, blk_l, cl = other(i)
        to_sib(blk_r, cr, sib_send.at[0, i], sib_recv.at[0, i]).wait_recv()
        to_sib(blk_l, cl, sib_send.at[1, i], sib_recv.at[1, i]).wait_recv()

    def pair(blk_a, ca, blk_b, cb):
        return (blk_a, ca), (blk_b, cb)

    def body(i, carry):
        comm(i)
        sib_wait(i - 1)
        attend(*pair(*other(i - 1)), *pair(*came(i)))
        return carry

    attend(*pair(*came(0)))
    lax.fori_loop(1, SENDS, body, 0)
    sib_wait(SENDS - 1)
    attend(*pair(*other(SENDS - 1)))

    total = jnp.zeros((8, C), F32)
    square = jnp.zeros((8, C), F32)
    for t in range(2):
        rows = pl.ds(256 * t, 256)
        inv = 1.0 / jnp.sum(l_s[rows, :], axis=1, keepdims=True)
        att = ((acc[rows, :] * inv - mean) * scale + shift).astype(BF16)
        x = jnp.concatenate([kv[me, 2 * t], kv[me, 2 * t + 1]], axis=0).astype(F32)
        h = (x + dot(att, wv[...])).astype(BF16)
        hid[2 * t] = h[:CH]
        hid[2 * t + 1] = h[CH:]
        h = h.astype(F32)
        if t == 0:
            base = h[0:1, :]
        a, b = sums_about(base, h)
        total = total + a
        square = square + b

    def halo_copy(k, row, peer):
        return pltpu.make_async_remote_copy(
            src_ref=hid.at[row],
            dst_ref=halo.at[k],
            send_sem=h_send.at[k],
            recv_sem=h_recv.at[k],
            device_id={"row": peer},
        )

    down = halo_copy(0, ROWS - 1, (me + 1) % DEV)
    up = halo_copy(1, 0, (me + DEV - 1) % DEV)
    put_moments(base, total, square, mine)
    for d in range(1, DEV):
        stat_copy(d, stat_b, sb_send, sb_recv).start()
    down.start()
    up.start()
    for c in taps:
        c.wait()
    down.wait()
    up.wait()
    for d in range(1, DEV):
        stat_copy(d, stat_b, sb_send, sb_recv).wait()
    mean2, rs2 = combined(stat_b, mine)
    coef[0] = mean2
    coef[1] = rs2 * vecs[2] * 0.5
    coef[2] = vecs[3] * 0.5
    edges[...] = halo[...]

    def drain(i, carry):
        blk_r, cr, blk_l, cl = came(i)
        ring(0, blk_r, cr, i).wait_send()
        ring(1, blk_l, cl, i).wait_send()
        to_sib(blk_r, cr, sib_send.at[0, i], sib_recv.at[0, i]).wait_send()
        to_sib(blk_l, cl, sib_send.at[1, i], sib_recv.at[1, i]).wait_send()
        return carry

    lax.fori_loop(0, SENDS, drain, 0)
    for i in range(4):
        to_sib(me, i, own_send.at[i], own_recv.at[i]).wait_send()


def conv_kernel(hid, edges, coef, wc, bias, out_ref, lhs):
    me = lax.axis_index("row")
    mean, scale, shift = coef[0], coef[1], coef[2]
    for j in range(ROWS + 2):
        src = edges[0] if j == 0 else edges[1] if j == ROWS + 1 else hid[j - 1]
        half = (src.astype(F32) - mean) * scale + shift
        act = half + half * jnp.tanh(half)
        if j == 0:
            act = jnp.where(me == 0, 0.0, act)
        if j == ROWS + 1:
            act = jnp.where(me == DEV - 1, 0.0, act)
        act = act.astype(BF16)
        for dy in range(3):
            i = j - dy
            if 0 <= i < ROWS:
                lhs[CH * i : CH * i + CH, C * dy : C * dy + C] = act

    col = lax.broadcasted_iota(jnp.int32, (N, 256), 0) % W
    for n in range(2):
        cols = slice(256 * n, 256 * n + 256)
        t0 = dot(lhs[...], wc[0, :, cols])
        t1 = dot(lhs[...], wc[1, :, cols])
        t2 = dot(lhs[...], wc[2, :, cols])
        total = t1 + jnp.where(col == 0, 0.0, pltpu.roll(t0, 1, 0))
        total = total + jnp.where(col == W - 1, 0.0, pltpu.roll(t2, N - 1, 0))
        base = jnp.concatenate([hid[i, :, cols] for i in range(4)], axis=0).astype(F32)
        out_ref[:, cols] = (base + (total + bias[:, cols])).astype(BF16)


def local(
    latent, attn_gain, attn_shift, w_query, w_key, w_value, w_out,
    conv_gain, conv_shift, w_conv, conv_bias,
):
    line = lambda v: v.reshape(1, C)
    dma = pltpu.SemaphoreType.DMA
    vmem = pl.BlockSpec(memory_space=pltpu.VMEM)
    hid, edges, coef, taps = pl.pallas_call(
        kernel,
        out_shape=(
            pltpu.VMEM((ROWS, W, C), BF16),
            pltpu.VMEM((2, W, C), BF16),
            pltpu.VMEM((3, 1, C), F32),
            pltpu.VMEM((3, 3 * C, C), BF16),
        ),
        in_specs=[pl.BlockSpec(memory_space=pltpu.HBM)] * 10,
        out_specs=(vmem,) * 4,
        scratch_shapes=[
            pltpu.VMEM((DEV, 4, CH, C), BF16),
            pltpu.VMEM((C, C), BF16),
            pltpu.VMEM((C, C), BF16),
            pltpu.VMEM((C, C), BF16),
            pltpu.VMEM((C, C), BF16),
            pltpu.VMEM((4, 1, C), F32),
            pltpu.VMEM((N, C), BF16),
            pltpu.VMEM((N, C), F32),
            pltpu.VMEM((N, 128), F32),
            pltpu.VMEM((N, 128), F32),
            pltpu.VMEM((2, W, C), BF16),
            pltpu.VMEM((8, 128), F32),
            pltpu.VMEM((DEV - 1, 8, 128), F32),
            pltpu.VMEM((DEV - 1, 8, 128), F32),
            dma((4,)),
            dma((4,)),
            dma((9,)),
            dma((4,)),
            dma((2, SENDS)),
            dma((2, SENDS)),
            dma((2, SENDS)),
            dma((2, SENDS)),
            dma((4,)),
            dma((4,)),
            dma((DEV - 1,)),
            dma((DEV - 1,)),
            dma((DEV - 1,)),
            dma((DEV - 1,)),
            dma((2,)),
            dma((2,)),
            pltpu.SemaphoreType.REGULAR((3,)),
        ],
        compiler_params=pltpu.CompilerParams(
            collective_id=0, has_side_effects=True, vmem_limit_bytes=28 * 1024 * 1024
        ),
    )(
        *(
            pltpu.with_memory_space_constraint(v, pltpu.HBM)
            for v in (
                latent.reshape(N, C), line(attn_gain), line(attn_shift), w_query, w_key,
                w_value, w_out, line(conv_gain), line(conv_shift), w_conv,
            )
        )
    )
    out = pl.pallas_call(
        conv_kernel,
        out_shape=jax.ShapeDtypeStruct((N, C), BF16),
        in_specs=[vmem] * 5,
        out_specs=vmem,
        scratch_shapes=[pltpu.VMEM((N, 3 * C), BF16)],
        compiler_params=pltpu.CompilerParams(vmem_limit_bytes=28 * 1024 * 1024),
    )(hid, edges, coef, taps, line(conv_bias))
    return out.reshape(ROWS, W, C)


def solution(mesh):
    part = P(("img", "row"), None, None)
    return jax.shard_map(
        local, mesh=mesh, in_specs=(part,) + (P(),) * 10, out_specs=part, check_vma=False
    )
```

time: 68.4 us -> 62.6 us (0.915)
  Pallas kernels: 66.4 us -> 62.5 us
  local copies, waits for them, and re-layouts: 1.87 us -> 0.01 us
    pallas_call x1 -> x2, Pallas kernels: 66.4 us -> 62.5 us  [the longest x1 59.1 us: local(): pl.pallas_call(kernel, out_shape=(pltpu.VMEM((ROWS, W, C), BF16), pltpu.V...]
    unnamed x1 -> x2, local copies, waits for them, and re-layouts: 1.87 us -> 0.01 us
where the time goes in v2:
time: 62.6 us; the launch traced here: 62.5 us
  Pallas kernels  62.5 us (100%)
    pallas_call x1, Pallas kernels, local(): pl.pallas_call(kernel, out_shape=(pltpu.VMEM((ROWS, W, C), BF16), pltpu.V...  59.1 us
    pallas_call x1, Pallas kernels, local(): pl.pallas_call(conv_kernel, out_shape=jax.ShapeDtypeStruct((N, C), BF16),...  3.42 us

profile of v2, /device:TPU:1, one launch (start us, length us, event | category | flops | bytes accessed | tf_op | source)
XLA Modules:
  0.0 62.5 jit_solution(1633877198063764022)
XLA Ops:
  0.0 0.0 copy-start
  0.0 59.1 %shard_map.109 = (bf16[4,128,512]{2,1,0:T(8,128)(2,1)S(1)}, bf16[2,128,512]{2,1,0:T(8,128)(2,1)S(1)}, f32[3,1,512]{2,1,0:T(1,128)S(1)}, bf16[3,1536,512]{2,1,0:T(8,128)(2,1)S(1)}) custom-call(bf16[512,512]{1,0:T(8,128)(2,1)} %bitcast.8, f32[1,512]{1,0:T(1,128)} %bitcast.9, f32[1,512]{1,0:T(1,128)} %bitcast.10, bf16[512,512]{1,0:T(8,128)(2,1)} %wq_h.1, ...), custom_call_target="tpu_custom_call" | custom-call | tf_op jit(solution)/shard_map/pallas_call | solution.py:371
  59.1 0.0 copy-done
  59.1 3.4 %shard_map.110 = bf16[512,512]{1,0:T(8,128)(2,1)} custom-call(bf16[4,128,512]{2,1,0:T(8,128)(2,1)S(1)} %get-tuple-element.9.hid, bf16[2,128,512]{2,1,0:T(8,128)(2,1)S(1)} %get-tuple-element.10.edges, f32[3,1,512]{2,1,0:T(1,128)S(1)} %get-tuple-element.11.coef, bf16[3,1536,512]{2,1,0:T(8,128)(2,1)S(1)} %get-tuple-element.12.wc, f32[1,512]{1,0:T(1,128)S(1)} %bitcast.7), custom_call_target="tpu_custom_call" | custom-call | tf_op jit(solution)/shard_map/pallas_call | solution.py:426
Async XLA Ops:
  0.0 59.1 %copy-start = (f32[512]{0:T(512)S(1)}, f32[512]{0:T(512)}, u32[]{:S(2)}) copy-start(f32[512]{0:T(512)} %param.21) | copy-start | bytes 6148

commit v3 on v2

--- a/solution.py
+++ b/solution.py
@@ -15,6 +15,7 @@
 ZN = 8
 SENDS = 14
 TILE = 256
+SPLIT = 2
 EPS = 1e-06
 F32 = jnp.float32
 BF16 = jnp.bfloat16
@@ -27,19 +28,41 @@
     return lax.dot_general(a, b, dims, preferred_element_type=F32)
 
 
+def as_rows(v):
+    return jnp.concatenate([v[:, 128 * i : 128 * i + 128] for i in range(4)], axis=0)
+
+
 def as_line(v):
     return jnp.concatenate([v[i : i + 1, :] for i in range(4)], axis=1)
+
+
+def partner(v, step):
+    lane = lax.broadcasted_iota(jnp.int32, v.shape, 1)
+    return jnp.where(
+        (lane // step) % 2 == 0, pltpu.roll(v, 128 - step, 1), pltpu.roll(v, step, 1)
+    )
+
+
+def slot(shape, first=0):
+    lane = lax.broadcasted_iota(jnp.int32, shape, 1)
+    return lane % GROUP == lax.broadcasted_iota(jnp.int32, shape, 0) + first
 
 
 def put_moments(first, total, square, buf):
     total = jnp.sum(total, axis=0, keepdims=True)
     square = jnp.sum(square, axis=0, keepdims=True)
     off = total * (1.0 / N)
-    dev = jnp.maximum(square - total * off, 0.0)
-    mean = first + off
-    for i in range(4):
-        buf[i : i + 1, :] = mean[:, 128 * i : 128 * i + 128]
-        buf[4 + i : 5 + i, :] = dev[:, 128 * i : 128 * i + 128]
+    dev = as_rows(jnp.maximum(square - total * off, 0.0))
+    mean = as_rows(first + off)
+    step, count = 1, float(N)
+    while step < GROUP:
+        other = partner(mean, step)
+        gap = other - mean
+        dev = dev + partner(dev, step) + (0.5 * count) * (gap * gap)
+        mean = 0.5 * (mean + other)
+        step, count = 2 * step, 2.0 * count
+    line = jnp.where(slot(mean.shape), mean, 0.0) + jnp.where(slot(dev.shape, 4), dev, 0.0)
+    buf[...] = jnp.sum(line, axis=0, keepdims=True)
 
 
 def sums_about(first, block):
@@ -48,27 +71,23 @@
 
 
 def combined(stats, own):
-    means = [own[0:4, :]] + [stats[i, 0:4, :] for i in range(DEV - 1)]
-    devs = [own[4:8, :]] + [stats[i, 4:8, :] for i in range(DEV - 1)]
-    centre = sum(means[1:], means[0]) * (1.0 / DEV)
-    spread = jnp.zeros((4, 128), F32)
-    for m, d in zip(means, devs):
-        off = m - centre
-        spread = spread + (d + float(N) * (off * off))
-    lane = lax.broadcasted_iota(jnp.int32, (4, 128), 1)
-    count = float(N * DEV)
+    lines = [own[...]] + [stats[i] for i in range(DEV - 1)]
+    total = sum(lines[1:], lines[0])
+    centre = total * (1.0 / DEV)
+    spread = jnp.zeros((1, 128), F32)
+    for v in lines:
+        off = v - centre
+        spread = spread + off * off
+    spread = pltpu.roll(total, 128 - 4, 1) + float(N * GROUP) * spread
+    rs = lax.rsqrt(spread * (1.0 / (DEV * GROUP * N)) + EPS)
+    rows = [
+        jnp.where(slot((4, 128)), jnp.broadcast_to(v, (4, 128)), 0.0) for v in (centre, rs)
+    ]
     step = 1
     while step < GROUP:
-        low = (lane // step) % 2 == 0
-        both = []
-        for v in (centre, spread):
-            both.append(jnp.where(low, pltpu.roll(v, 128 - step, 1), pltpu.roll(v, step, 1)))
-        gap = both[0] - centre
-        spread = spread + both[1] + (0.5 * count) * (gap * gap)
-        centre = 0.5 * (centre + both[0])
+        rows = [v + partner(v, step) for v in rows]
         step *= 2
-        count *= 2.0
-    return as_line(centre), as_line(lax.rsqrt(spread * (1.0 / count) + EPS))
+    return tuple(as_line(v) for v in rows)
 
 
 def kernel(
@@ -155,8 +174,9 @@
     ring(1, me, 2, 0).start()
     loads[1].wait()
     loads[3].wait()
-    ring(0, me, 1, 1).start()
-    ring(1, me, 3, 1).start()
+    for j in range(1, 3):
+        ring(0, me, order[j][0], j).start()
+        ring(1, me, order[j][1], j).start()
 
     far_right = ((z + 2) % ZN) * 2 + core
     far_left = ((z + ZN - 2) % ZN) * 2 + core
@@ -171,7 +191,7 @@
 
     for d in range(1, DEV):
         stat_copy(d, stat_a, sa_send, sa_recv).start()
-    for j in range(2, 4):
+    for j in range(3, 4):
         ring(0, me, order[j][0], j).start()
         ring(1, me, order[j][1], j).start()
     for i in range(4):
@@ -232,6 +252,7 @@
         c.wait()
     for d in range(1, DEV):
         stat_copy(d, stat_a, sa_send, sa_recv).wait()
+    comm(1)
     mean, rs = combined(stat_a, mine)
     scale = rs * vecs[0]
     shift = vecs[1]
@@ -264,53 +285,59 @@
         return (blk_a, ca), (blk_b, cb)
 
     def body(i, carry):
-        comm(i)
+        pl.when(i > 2)(lambda: comm(i))
         sib_wait(i - 1)
         attend(*pair(*other(i - 1)), *pair(*came(i)))
         return carry
 
+    comm(2)
     attend(*pair(*came(0)))
     lax.fori_loop(1, SENDS, body, 0)
     sib_wait(SENDS - 1)
     attend(*pair(*other(SENDS - 1)))
 
+    def halo_copy(k, part):
+        row, peer = ((ROWS - 1, (me + 1) % DEV), (0, (me + DEV - 1) % DEV))[k]
+        piece = pl.ds(part * (W // 2), W // 2)
+        return pltpu.make_async_remote_copy(
+            src_ref=hid.at[row, piece],
+            dst_ref=halo.at[k, piece],
+            send_sem=h_send.at[k, part],
+            recv_sem=h_recv.at[k, part],
+            device_id={"row": peer},
+        )
+
     total = jnp.zeros((8, C), F32)
     square = jnp.zeros((8, C), F32)
-    for t in range(2):
-        rows = pl.ds(256 * t, 256)
-        inv = 1.0 / jnp.sum(l_s[rows, :], axis=1, keepdims=True)
-        att = ((acc[rows, :] * inv - mean) * scale + shift).astype(BF16)
-        x = jnp.concatenate([kv[me, 2 * t], kv[me, 2 * t + 1]], axis=0).astype(F32)
+    for pair_rows in ((0, 3), (1, 2)):
+        spans = [pl.ds(W * r, W) for r in pair_rows]
+        den = jnp.concatenate([l_s[rows, :] for rows in spans], axis=0)
+        inv = 1.0 / jnp.sum(den, axis=1, keepdims=True)
+        got = jnp.concatenate([acc[rows, :] for rows in spans], axis=0)
+        att = ((got * inv - mean) * scale + shift).astype(BF16)
+        x = jnp.concatenate([kv[me, r] for r in pair_rows], axis=0).astype(F32)
         h = (x + dot(att, wv[...])).astype(BF16)
-        hid[2 * t] = h[:CH]
-        hid[2 * t + 1] = h[CH:]
+        hid[pair_rows[0]] = h[:W]
+        hid[pair_rows[1]] = h[W:]
         h = h.astype(F32)
-        if t == 0:
+        if pair_rows[0] == 0:
             base = h[0:1, :]
+            for k in range(2):
+                halo_copy(k, 0).start()
         a, b = sums_about(base, h)
         total = total + a
         square = square + b
 
-    def halo_copy(k, row, peer):
-        return pltpu.make_async_remote_copy(
-            src_ref=hid.at[row],
-            dst_ref=halo.at[k],
-            send_sem=h_send.at[k],
-            recv_sem=h_recv.at[k],
-            device_id={"row": peer},
-        )
-
-    down = halo_copy(0, ROWS - 1, (me + 1) % DEV)
-    up = halo_copy(1, 0, (me + DEV - 1) % DEV)
     put_moments(base, total, square, mine)
     for d in range(1, DEV):
         stat_copy(d, stat_b, sb_send, sb_recv).start()
-    down.start()
-    up.start()
+    for k in range(2):
+        halo_copy(k, 1).start()
     for c in taps:
         c.wait()
-    down.wait()
-    up.wait()
+    for k in range(2):
+        for part in range(2):
+            halo_copy(k, part).wait()
     for d in range(1, DEV):
         stat_copy(d, stat_b, sb_send, sb_recv).wait()
     mean2, rs2 = combined(stat_b, mine)
@@ -332,10 +359,11 @@
         to_sib(me, i, own_send.at[i], own_recv.at[i]).wait_send()
 
 
-def conv_kernel(hid, edges, coef, wc, bias, out_ref, lhs):
+def conv_kernel(hid, edges, coef, wc, bias, out_hbm, act_s, out_s, out_sem):
     me = lax.axis_index("row")
     mean, scale, shift = coef[0], coef[1], coef[2]
-    for j in range(ROWS + 2):
+
+    def activate(j):
         src = edges[0] if j == 0 else edges[1] if j == ROWS + 1 else hid[j - 1]
         half = (src.astype(F32) - mean) * scale + shift
         act = half + half * jnp.tanh(half)
@@ -343,22 +371,33 @@
             act = jnp.where(me == 0, 0.0, act)
         if j == ROWS + 1:
             act = jnp.where(me == DEV - 1, 0.0, act)
-        act = act.astype(BF16)
-        for dy in range(3):
-            i = j - dy
-            if 0 <= i < ROWS:
-                lhs[CH * i : CH * i + CH, C * dy : C * dy + C] = act
-
-    col = lax.broadcasted_iota(jnp.int32, (N, 256), 0) % W
-    for n in range(2):
-        cols = slice(256 * n, 256 * n + 256)
-        t0 = dot(lhs[...], wc[0, :, cols])
-        t1 = dot(lhs[...], wc[1, :, cols])
-        t2 = dot(lhs[...], wc[2, :, cols])
-        total = t1 + jnp.where(col == 0, 0.0, pltpu.roll(t0, 1, 0))
-        total = total + jnp.where(col == W - 1, 0.0, pltpu.roll(t2, N - 1, 0))
-        base = jnp.concatenate([hid[i, :, cols] for i in range(4)], axis=0).astype(F32)
-        out_ref[:, cols] = (base + (total + bias[:, cols])).astype(BF16)
+        act_s[W * j : W * j + W, :] = act.astype(BF16)
+
+    part = N // SPLIT
+    col = lax.broadcasted_iota(jnp.int32, (part, C), 0) % W
+    ready = 0
+    copies = []
+    for m in range(SPLIT):
+        rows = slice(part * m, part * m + part)
+        while ready * W < part * m + part + 2 * W:
+            activate(ready)
+            ready += 1
+        t = [
+            sum(
+                dot(act_s[part * m + W * dy : part * m + W * dy + part, :], wc[dx, C * dy : C * dy + C])
+                for dy in range(3)
+            )
+            for dx in range(3)
+        ]
+        total = t[1] + jnp.where(col == 0, 0.0, pltpu.roll(t[0], 1, 0))
+        total = total + jnp.where(col == W - 1, 0.0, pltpu.roll(t[2], part - 1, 0))
+        first = part // W * m
+        base = jnp.concatenate([hid[first + i] for i in range(part // W)], axis=0).astype(F32)
+        out_s[rows, :] = (base + (total + bias[...])).astype(BF16)
+        copies.append(pltpu.make_async_copy(out_s.at[rows], out_hbm.at[rows], out_sem.at[m]))
+        copies[-1].start()
+    for c in copies:
+        c.wait()
 
 
 def local(
@@ -390,9 +429,9 @@
             pltpu.VMEM((N, 128), F32),
             pltpu.VMEM((N, 128), F32),
             pltpu.VMEM((2, W, C), BF16),
-            pltpu.VMEM((8, 128), F32),
-            pltpu.VMEM((DEV - 1, 8, 128), F32),
-            pltpu.VMEM((DEV - 1, 8, 128), F32),
+            pltpu.VMEM((1, 128), F32),
+            pltpu.VMEM((DEV - 1, 1, 128), F32),
+            pltpu.VMEM((DEV - 1, 1, 128), F32),
             dma((4,)),
             dma((4,)),
             dma((9,)),
@@ -407,8 +446,8 @@
             dma((DEV - 1,)),
             dma((DEV - 1,)),
             dma((DEV - 1,)),
-            dma((2,)),
-            dma((2,)),
+            dma((2, 2)),
+            dma((2, 2)),
             pltpu.SemaphoreType.REGULAR((3,)),
         ],
         compiler_params=pltpu.CompilerParams(
@@ -427,8 +466,12 @@
         conv_kernel,
         out_shape=jax.ShapeDtypeStruct((N, C), BF16),
         in_specs=[vmem] * 5,
-        out_specs=vmem,
-        scratch_shapes=[pltpu.VMEM((N, 3 * C), BF16)],
+        out_specs=pl.BlockSpec(memory_space=pltpu.HBM),
+        scratch_shapes=[
+            pltpu.VMEM((N + 2 * W, C), BF16),
+            pltpu.VMEM((N, C), BF16),
+            dma((SPLIT,)),
+        ],
         compiler_params=pltpu.CompilerParams(vmem_limit_bytes=28 * 1024 * 1024),
     )(hid, edges, coef, taps, line(conv_bias))
     return out.reshape(ROWS, W, C)

time: 62.6 us -> 61.3 us (0.979)
  Pallas kernels: 62.5 us -> 61.2 us
    pallas_call x1, Pallas kernels: 59.1 us -> 57.7 us  [local(): pl.pallas_call(kernel, out_shape=(pltpu.VMEM((ROWS, W, C), BF16), pltpu.V...]
where the time goes in v3:
time: 61.3 us; the launch traced here: 61.2 us
  Pallas kernels  61.2 us (100%)
    pallas_call x1, Pallas kernels, local(): pl.pallas_call(kernel, out_shape=(pltpu.VMEM((ROWS, W, C), BF16), pltpu.V...  57.7 us
    pallas_call x1, Pallas kernels, local(): pl.pallas_call(conv_kernel, out_shape=jax.ShapeDtypeStruct((N, C), BF16),...  3.49 us

profile of v3, /device:TPU:1, one launch (start us, length us, event | category | flops | bytes accessed | tf_op | source)
XLA Modules:
  0.0 61.2 jit_solution(4774735769634963679)
XLA Ops:
  0.0 0.0 copy-start
  0.0 57.7 %shard_map.109 = (bf16[4,128,512]{2,1,0:T(8,128)(2,1)S(1)}, bf16[2,128,512]{2,1,0:T(8,128)(2,1)S(1)}, f32[3,1,512]{2,1,0:T(1,128)S(1)}, bf16[3,1536,512]{2,1,0:T(8,128)(2,1)S(1)}) custom-call(bf16[512,512]{1,0:T(8,128)(2,1)} %bitcast.8, f32[1,512]{1,0:T(1,128)} %bitcast.9, f32[1,512]{1,0:T(1,128)} %bitcast.10, bf16[512,512]{1,0:T(8,128)(2,1)} %wq_h.1, ...), custom_call_target="tpu_custom_call" | custom-call | tf_op jit(solution)/shard_map/pallas_call | solution.py:410
  57.7 0.0 copy-done
  57.7 3.5 %shard_map.110 = bf16[512,512]{1,0:T(8,128)(2,1)} custom-call(bf16[4,128,512]{2,1,0:T(8,128)(2,1)S(1)} %get-tuple-element.9.hid, bf16[2,128,512]{2,1,0:T(8,128)(2,1)S(1)} %get-tuple-element.10.edges, f32[3,1,512]{2,1,0:T(1,128)S(1)} %get-tuple-element.11.coef, bf16[3,1536,512]{2,1,0:T(8,128)(2,1)S(1)} %get-tuple-element.12.wc, f32[1,512]{1,0:T(1,128)S(1)} %bitcast.7), custom_call_target="tpu_custom_call" | custom-call | tf_op jit(solution)/shard_map/pallas_call | solution.py:465
Async XLA Ops:
  0.0 57.7 %copy-start = (f32[512]{0:T(512)S(1)}, f32[512]{0:T(512)}, u32[]{:S(2)}) copy-start(f32[512]{0:T(512)} %param.21) | copy-start | bytes 6148

commit v4 on v3

--- a/solution.py
+++ b/solution.py
@@ -16,6 +16,8 @@
 SENDS = 14
 TILE = 256
 SPLIT = 2
+FEW = 16
+NEAREST = sorted(range(1, DEV), key=lambda d: min(d, DEV - d))
 EPS = 1e-06
 F32 = jnp.float32
 BF16 = jnp.bfloat16
@@ -93,7 +95,7 @@
 def kernel(
     x_hbm, ag_h, as_h, wq_h, wk_h, wv_h, wo_h, cg_h, cs_h, wc_h,
     hid, edges, coef, wc,
-    kv, wq, wk, wv, wo, vecs, q_s, acc, m_s, l_s, halo, mine, stat_a, stat_b,
+    kv, wq, wk, wv, wo, mid, vecs, q_s, acc, m_s, l_s, halo, mine, stat_a, stat_b,
     load_sem, w_sem, wc_sem, v_sem,
     ring_send, ring_recv, sib_send, sib_recv, own_send, own_recv,
     sa_send, sa_recv, sb_send, sb_recv, h_send, h_recv, known,
@@ -109,34 +111,27 @@
         pltpu.make_async_copy(x_hbm.at[pl.ds(CH * i, CH)], kv.at[me, i], load_sem.at[i])
         for i in range(4)
     ]
-    for c in loads:
-        c.start()
-
     barrier = pltpu.get_barrier_semaphore()
     for peer in (left, right, sib):
         pl.semaphore_signal(barrier, inc=1, device_id={"row": peer})
+    for c in loads:
+        c.start()
 
     small = [
         pltpu.make_async_copy(src, vecs.at[i], v_sem.at[i])
         for i, src in enumerate((ag_h, as_h, cg_h, cs_h))
     ]
-    for c in small:
-        c.start()
     weights = [
         pltpu.make_async_copy(src, dst, w_sem.at[i])
         for i, (src, dst) in enumerate(((wq_h, wq), (wk_h, wk), (wv_h, wv), (wo_h, wo)))
     ]
-    for c in weights:
-        c.start()
     taps = [
         pltpu.make_async_copy(
-            wc_h.at[dy, dx], wc.at[dx, pl.ds(C * dy, C)], wc_sem.at[3 * dy + dx]
+            wc_h.at[dy, dx], (wc.at[dx, 0], mid.at[dx], wc.at[dx, 3])[dy], wc_sem.at[3 * dy + dx]
         )
         for dy in range(3)
         for dx in range(3)
     ]
-    for c in taps:
-        c.start()
 
     def ring(way, blk, chunk, j):
         return pltpu.make_async_remote_copy(
@@ -178,6 +173,9 @@
         ring(0, me, order[j][0], j).start()
         ring(1, me, order[j][1], j).start()
 
+    for c in (*small, *weights):
+        c.start()
+
     far_right = ((z + 2) % ZN) * 2 + core
     far_left = ((z + ZN - 2) % ZN) * 2 + core
     for k, peers in enumerate(((left, right, sib), (far_left, far_right), (sib,))):
@@ -214,16 +212,14 @@
 
     def comm(i):
         blk_r, cr, blk_l, cl = came(i)
-        ring(0, blk_r, cr, i).wait_recv()
-        ring(1, blk_l, cl, i).wait_recv()
-
-        @pl.when(i < SENDS - 4)
-        def _():
-            ring(0, blk_r, cr, i + 4).start()
-            ring(1, blk_l, cl, i + 4).start()
-
-        to_sib(blk_r, cr, sib_send.at[0, i], sib_recv.at[0, i]).start()
-        to_sib(blk_l, cl, sib_send.at[1, i], sib_recv.at[1, i]).start()
+        for way, blk, chunk in ((0, blk_r, cr), (1, blk_l, cl)):
+            ring(way, blk, chunk, i).wait_recv()
+
+            @pl.when(i < SENDS - 4)
+            def _():
+                ring(way, blk, chunk, i + 4).start()
+
+            to_sib(blk, chunk, sib_send.at[way, i], sib_recv.at[way, i]).start()
 
     def attend(*chunks):
         keys = jnp.concatenate([kv[blk, chunk] for blk, chunk in chunks], axis=0)
@@ -270,6 +266,8 @@
         attend((blk, 0), (blk, 1), (blk, 2), (blk, 3))
         return carry
 
+    for c in taps:
+        c.start()
     lax.fori_loop(0, 2, first, 0)
 
     def other(i):
@@ -284,7 +282,22 @@
     def pair(blk_a, ca, blk_b, cb):
         return (blk_a, ca), (blk_b, cb)
 
+    def spread_taps(k):
+        dx, rows = k // 8, pl.ds(pl.multiple_of(k % 8 * 64, 64), 64)
+        ends = (wc[dx, 0, rows, :].astype(F32) + wc[dx, 3, rows, :].astype(F32)) * -0.5
+        half = mid[dx, rows, :].astype(F32) * -0.5
+        wc[dx, 1, rows, :] = (ends + half).astype(BF16)
+        wc[dx, 2, rows, :] = (ends - half).astype(BF16)
+
+    for c in taps:
+        c.wait()
+
     def body(i, carry):
+        @pl.when(i < 13)
+        def _():
+            spread_taps(2 * i - 2)
+            spread_taps(2 * i - 1)
+
         pl.when(i > 2)(lambda: comm(i))
         sib_wait(i - 1)
         attend(*pair(*other(i - 1)), *pair(*came(i)))
@@ -333,19 +346,6 @@
         stat_copy(d, stat_b, sb_send, sb_recv).start()
     for k in range(2):
         halo_copy(k, 1).start()
-    for c in taps:
-        c.wait()
-    for k in range(2):
-        for part in range(2):
-            halo_copy(k, part).wait()
-    for d in range(1, DEV):
-        stat_copy(d, stat_b, sb_send, sb_recv).wait()
-    mean2, rs2 = combined(stat_b, mine)
-    coef[0] = mean2
-    coef[1] = rs2 * vecs[2] * 0.5
-    coef[2] = vecs[3] * 0.5
-    edges[...] = halo[...]
-
     def drain(i, carry):
         blk_r, cr, blk_l, cl = came(i)
         ring(0, blk_r, cr, i).wait_send()
@@ -358,43 +358,66 @@
     for i in range(4):
         to_sib(me, i, own_send.at[i], own_recv.at[i]).wait_send()
 
-
-def conv_kernel(hid, edges, coef, wc, bias, out_hbm, act_s, out_s, out_sem):
+    for k in range(2):
+        for part in range(2):
+            halo_copy(k, part).wait_send()
+    for d in range(1, DEV):
+        stat_copy(d, stat_b, sb_send, sb_recv).wait_send()
+    for d in NEAREST:
+        stat_copy(d, stat_b, sb_send, sb_recv).wait_recv()
+    for k in range(2):
+        for part in range(2):
+            halo_copy(k, part).wait_recv()
+    edges[...] = halo[...]
+    mean2, rs2 = combined(stat_b, mine)
+    coef[0] = mean2
+    coef[1] = rs2 * vecs[2] * 0.5
+    coef[2] = vecs[3] * 0.5
+
+
+def conv_kernel(hid, edges, coef, wc, bias, out_hbm, mix_s, out_s, out_sem):
     me = lax.axis_index("row")
     mean, scale, shift = coef[0], coef[1], coef[2]
 
-    def activate(j):
-        src = edges[0] if j == 0 else edges[1] if j == ROWS + 1 else hid[j - 1]
-        half = (src.astype(F32) - mean) * scale + shift
-        act = half + half * jnp.tanh(half)
-        if j == 0:
-            act = jnp.where(me == 0, 0.0, act)
-        if j == ROWS + 1:
-            act = jnp.where(me == DEV - 1, 0.0, act)
-        act_s[W * j : W * j + W, :] = act.astype(BF16)
-
-    part = N // SPLIT
-    col = lax.broadcasted_iota(jnp.int32, (part, C), 0) % W
-    ready = 0
+    for lo in range(0, W, FEW):
+        d = []
+        for j in range(ROWS + 2):
+            src, r = (edges, 0) if j == 0 else (edges, 1) if j == ROWS + 1 else (hid, j - 1)
+            half = (src[r, lo : lo + FEW, :].astype(F32) - mean) * scale + shift
+            act = half + half * jnp.tanh(half)
+            if j == 0:
+                act = jnp.where(me == 0, 0.0, act)
+            if j == ROWS + 1:
+                act = jnp.where(me == DEV - 1, 0.0, act)
+            d.append(act.astype(BF16))
+        for a in range(2):
+            e = d[2 * a : 2 * a + 4]
+            for k, v in ((1, e[1] + e[2]), (2, e[2] - e[1]), (0, e[0] - e[2]), (3, e[1] - e[3])):
+                mix_s[k, W * a + lo : W * a + lo + FEW, :] = v
+
+    part = C // SPLIT
+    col = lax.broadcasted_iota(jnp.int32, (2 * W, part), 0) % W
     copies = []
-    for m in range(SPLIT):
-        rows = slice(part * m, part * m + part)
-        while ready * W < part * m + part + 2 * W:
-            activate(ready)
-            ready += 1
-        t = [
-            sum(
-                dot(act_s[part * m + W * dy : part * m + W * dy + part, :], wc[dx, C * dy : C * dy + C])
-                for dy in range(3)
-            )
-            for dx in range(3)
-        ]
-        total = t[1] + jnp.where(col == 0, 0.0, pltpu.roll(t[0], 1, 0))
-        total = total + jnp.where(col == W - 1, 0.0, pltpu.roll(t[2], part - 1, 0))
-        first = part // W * m
-        base = jnp.concatenate([hid[first + i] for i in range(part // W)], axis=0).astype(F32)
-        out_s[rows, :] = (base + (total + bias[...])).astype(BF16)
-        copies.append(pltpu.make_async_copy(out_s.at[rows], out_hbm.at[rows], out_sem.at[m]))
+    for n in range(SPLIT):
+        cols = slice(part * n, part * n + part)
+        rows = [None, None]
+        for dx in (1, 0, 2):
+            m = [None] * 4
+            for k in (1, 2, 0, 3):
+                m[k] = dot(mix_s[k], wc[dx, k, :, cols])
+            for i, v in enumerate((m[0] - m[1] - m[2], m[2] - m[1] - m[3])):
+                if dx == 0:
+                    v = jnp.where(col == 0, 0.0, pltpu.roll(v, 1, 0))
+                if dx == 2:
+                    v = jnp.where(col == W - 1, 0.0, pltpu.roll(v, 2 * W - 1, 0))
+                rows[i] = v if rows[i] is None else rows[i] + v
+        for r in range(ROWS):
+            total = rows[r % 2][W * (r // 2) : W * (r // 2) + W]
+            base = hid[r, :, cols].astype(F32)
+            out_s[W * r : W * r + W, cols] = (base + (total + bias[:, cols])).astype(BF16)
+        copies.append(
+            pltpu.make_async_copy(out_s.at[:, cols], out_hbm.at[:, cols], out_sem.at[n])
+        )
         copies[-1].start()
     for c in copies:
         c.wait()
@@ -413,7 +436,7 @@
             pltpu.VMEM((ROWS, W, C), BF16),
             pltpu.VMEM((2, W, C), BF16),
             pltpu.VMEM((3, 1, C), F32),
-            pltpu.VMEM((3, 3 * C, C), BF16),
+            pltpu.VMEM((3, 4, C, C), BF16),
         ),
         in_specs=[pl.BlockSpec(memory_space=pltpu.HBM)] * 10,
         out_specs=(vmem,) * 4,
@@ -423,6 +446,7 @@
             pltpu.VMEM((C, C), BF16),
             pltpu.VMEM((C, C), BF16),
             pltpu.VMEM((C, C), BF16),
+            pltpu.VMEM((3, C, C), BF16),
             pltpu.VMEM((4, 1, C), F32),
             pltpu.VMEM((N, C), BF16),
             pltpu.VMEM((N, C), F32),
@@ -451,7 +475,7 @@
             pltpu.SemaphoreType.REGULAR((3,)),
         ],
         compiler_params=pltpu.CompilerParams(
-            collective_id=0, has_side_effects=True, vmem_limit_bytes=28 * 1024 * 1024
+            collective_id=0, has_side_effects=True, vmem_limit_bytes=30 * 1024 * 1024
         ),
     )(
         *(
@@ -468,7 +492,7 @@
         in_specs=[vmem] * 5,
         out_specs=pl.BlockSpec(memory_space=pltpu.HBM),
         scratch_shapes=[
-            pltpu.VMEM((N + 2 * W, C), BF16),
+            pltpu.VMEM((4, 2 * W, C), BF16),
             pltpu.VMEM((N, C), BF16),
             dma((SPLIT,)),
         ],

time: 61.3 us -> 60.8 us (level)
  no operation moved by 1% of the time
where the time goes in v4:
time: 60.8 us; the launch traced here: 60.7 us
  Pallas kernels  60.7 us (100%)
    pallas_call x1, Pallas kernels, local(): pl.pallas_call(kernel, out_shape=(pltpu.VMEM((ROWS, W, C), BF16), pltpu.V...  57.6 us
    pallas_call x1, Pallas kernels, local(): pl.pallas_call(conv_kernel, out_shape=jax.ShapeDtypeStruct((N, C), BF16),...  3.04 us

profile of v4, /device:TPU:1, one launch (start us, length us, event | category | flops | bytes accessed | tf_op | source)
XLA Modules:
  0.0 60.7 jit_solution(13774787670177385034)
XLA Ops:
  0.0 0.0 copy-start
  0.0 57.6 %shard_map.109 = (bf16[4,128,512]{2,1,0:T(8,128)(2,1)S(1)}, bf16[2,128,512]{2,1,0:T(8,128)(2,1)S(1)}, f32[3,1,512]{2,1,0:T(1,128)S(1)}, bf16[3,4,512,512]{3,2,1,0:T(8,128)(2,1)S(1)}) custom-call(bf16[512,512]{1,0:T(8,128)(2,1)} %bitcast.8, f32[1,512]{1,0:T(1,128)} %bitcast.9, f32[1,512]{1,0:T(1,128)} %bitcast.10, bf16[512,512]{1,0:T(8,128)(2,1)} %wq_h.1, ...), custom_call_target="tpu_custom_call" | custom-call | tf_op jit(solution)/shard_map/pallas_call | solution.py:433
  57.6 0.0 copy-done
  57.7 3.0 %shard_map.110 = bf16[512,512]{1,0:T(8,128)(2,1)} custom-call(bf16[4,128,512]{2,1,0:T(8,128)(2,1)S(1)} %get-tuple-element.9.hid, bf16[2,128,512]{2,1,0:T(8,128)(2,1)S(1)} %get-tuple-element.10.edges, f32[3,1,512]{2,1,0:T(1,128)S(1)} %get-tuple-element.11.coef, bf16[3,4,512,512]{3,2,1,0:T(8,128)(2,1)S(1)} %get-tuple-element.12.wc, f32[1,512]{1,0:T(1,128)S(1)} %bitcast.7), custom_call_target="tpu_custom_call" | custom-call | tf_op jit(solution)/shard_map/pallas_call | solution.py:489
Async XLA Ops:
  0.0 57.6 %copy-start = (f32[512]{0:T(512)S(1)}, f32[512]{0:T(512)}, u32[]{:S(2)}) copy-start(f32[512]{0:T(512)} %param.21) | copy-start | bytes 6148

commit v5 on v4

--- a/solution.py
+++ b/solution.py
@@ -306,9 +306,6 @@
     comm(2)
     attend(*pair(*came(0)))
     lax.fori_loop(1, SENDS, body, 0)
-    sib_wait(SENDS - 1)
-    attend(*pair(*other(SENDS - 1)))
-
     def halo_copy(k, part):
         row, peer = ((ROWS - 1, (me + 1) % DEV), (0, (me + DEV - 1) % DEV))[k]
         piece = pl.ds(part * (W // 2), W // 2)
@@ -320,13 +317,27 @@
             device_id={"row": peer},
         )
 
+    sib_wait(SENDS - 1)
+    keys = jnp.concatenate([kv[blk, chunk] for blk, chunk in pair(*other(SENDS - 1))], axis=0)
+    tiles = ((0, 3), (1, 2))
+
+    def of(ref, pair_rows):
+        return jnp.concatenate([ref[W * r : W * r + W, :] for r in pair_rows], axis=0)
+
     total = jnp.zeros((8, C), F32)
     square = jnp.zeros((8, C), F32)
-    for pair_rows in ((0, 3), (1, 2)):
-        spans = [pl.ds(W * r, W) for r in pair_rows]
-        den = jnp.concatenate([l_s[rows, :] for rows in spans], axis=0)
+    s = dot(of(q_s, tiles[0]), keys, NT)
+    for t, pair_rows in enumerate(tiles):
+        ahead = dot(of(q_s, tiles[1]), keys, NT) if t == 0 else None
+        m_old = of(m_s, pair_rows)
+        m_new = jnp.maximum(m_old, jnp.max(s, axis=1, keepdims=True))
+        alpha = jnp.exp2(m_old - m_new)
+        p = [jnp.exp2(s[:, k : k + 128] - m_new).astype(BF16) for k in (0, 128)]
+        den = of(l_s, pair_rows) * alpha + (p[0].astype(F32) + p[1].astype(F32))
+        got = of(acc, pair_rows) * jnp.concatenate([alpha] * 4, axis=1)
+        got = got + dot(jnp.concatenate(p, axis=1), keys)
+        s = ahead
         inv = 1.0 / jnp.sum(den, axis=1, keepdims=True)
-        got = jnp.concatenate([acc[rows, :] for rows in spans], axis=0)
         att = ((got * inv - mean) * scale + shift).astype(BF16)
         x = jnp.concatenate([kv[me, r] for r in pair_rows], axis=0).astype(F32)
         h = (x + dot(att, wv[...])).astype(BF16)

time: 60.8 us -> 60.8 us (level)
  no operation moved by 1% of the time
where the time goes in v5:
time: 60.8 us; the launch traced here: 60.7 us
  Pallas kernels  60.6 us (100%)
    pallas_call x1, Pallas kernels, local(): pl.pallas_call(kernel, out_shape=(pltpu.VMEM((ROWS, W, C), BF16), pltpu.V...  57.6 us
    pallas_call x1, Pallas kernels, local(): pl.pallas_call(conv_kernel, out_shape=jax.ShapeDtypeStruct((N, C), BF16),...  3.04 us

profile of v5, /device:TPU:1, one launch (start us, length us, event | category | flops | bytes accessed | tf_op | source)
XLA Modules:
  0.0 60.7 jit_solution(1432444763990838463)
XLA Ops:
  0.0 0.0 copy-start
  0.0 57.6 %shard_map.109 = (bf16[4,128,512]{2,1,0:T(8,128)(2,1)S(1)}, bf16[2,128,512]{2,1,0:T(8,128)(2,1)S(1)}, f32[3,1,512]{2,1,0:T(1,128)S(1)}, bf16[3,4,512,512]{3,2,1,0:T(8,128)(2,1)S(1)}) custom-call(bf16[512,512]{1,0:T(8,128)(2,1)} %bitcast.8, f32[1,512]{1,0:T(1,128)} %bitcast.9, f32[1,512]{1,0:T(1,128)} %bitcast.10, bf16[512,512]{1,0:T(8,128)(2,1)} %wq_h.1, ...), custom_call_target="tpu_custom_call" | custom-call | tf_op jit(solution)/shard_map/pallas_call | solution.py:444
  57.6 0.0 copy-done
  57.6 3.0 %shard_map.110 = bf16[512,512]{1,0:T(8,128)(2,1)} custom-call(bf16[4,128,512]{2,1,0:T(8,128)(2,1)S(1)} %get-tuple-element.9.hid, bf16[2,128,512]{2,1,0:T(8,128)(2,1)S(1)} %get-tuple-element.10.edges, f32[3,1,512]{2,1,0:T(1,128)S(1)} %get-tuple-element.11.coef, bf16[3,4,512,512]{3,2,1,0:T(8,128)(2,1)S(1)} %get-tuple-element.12.wc, f32[1,512]{1,0:T(1,128)S(1)} %bitcast.7), custom_call_target="tpu_custom_call" | custom-call | tf_op jit(solution)/shard_map/pallas_call | solution.py:500
Async XLA Ops:
  0.0 57.6 %copy-start = (f32[512]{0:T(512)S(1)}, f32[512]{0:T(512)}, u32[]{:S(2)}) copy-start(f32[512]{0:T(512)} %param.21) | copy-start | bytes 6148
